TPU v7x, 32 devices: a whole 2x2x4 slice. The times are simulated.
32 devices in a mesh: dp: 16 (over z, y, core), mp: 2 (over x).
Axes of the slice: x: 2, y: 2, z: 4, core: 2. Of those that a mesh axis runs over, the one named last changes fastest.
Arguments:
- hidden: bfloat16 [512, 7168], P('dp', 'mp'), may hold values from -12 to 12
- steering: float32 [7168], P('mp'), may hold values from -3 to 3
- norm_gain: bfloat16 [7168], P('mp'), may hold values from 0.099609375 to 1.8984375
- target: bfloat16 [512, 7168], P('dp', 'mp'), may hold values from -8 to 8
- routes: int32 [512, 8], P('dp'), may hold values from 0 to 15, all different within a row; in each aligned block of 32 rows (0 to 31, 32 to 63, ...) at most 20 rows name the same one
- gate_probs: float32 [512, 8], P('dp'), may hold values from 0.05 to 0.3
- contrast: int32 [512], P('dp'), may hold values from 0 to 1
- gate_weight: bfloat16 [16, 7168, 2048], P('dp', None, 'mp'), may hold values from -0.0625 to 0.0625
- up_weight: bfloat16 [16, 7168, 2048], P('dp', None, 'mp'), may hold values from -0.0625 to 0.0625
- down_weight: bfloat16 [16, 2048, 7168], P('dp', 'mp'), may hold values from -0.125 to 0.125
Outputs:
- mixed: bfloat16 [512, 7168], P('dp', 'mp')
- steer_grad: float32 [7168], P('mp')
Inputs may be any that keep to these rules, and one draw needn't show every extreme that they name: `routes`: each row names 8 different experts; among the 32 rows of one index of dp no expert is named by more than 20 rows.
All inputs are finite; a program needn't handle non-finite values.
Results may differ from a plain program's by a relative error of at most 0.005.
Values may be sent and summed in bfloat16 or wider, within the bound.
No kernel may reach another device: no remote copies, remote signals or barrier semaphores. Data moves between devices by JAX's collectives and lax.ppermute only.
A program may use at most 128 MiB of HBM per device.

v0:
```python
import jax
import jax.numpy as jnp
from jax import lax
from jax.sharding import PartitionSpec as P

EPSILON = 1e-06


def expert_inputs(rows_in, grad_in, gate_mat, up_mat, down_mat):
    gate_pre = jnp.einsum("secd,edf->secf", rows_in, gate_mat, preferred_element_type=jnp.float32)
    up_pre = jnp.einsum("secd,edf->secf", rows_in, up_mat, preferred_element_type=jnp.float32)
    back_hidden = jnp.einsum(
        "secd,efd->secf", grad_in, down_mat, preferred_element_type=jnp.float32
    )
    return (gate_pre, up_pre, back_hidden)


def expert_outputs(gate_pre, up_pre, back_hidden, gate_mat, up_mat, down_mat):
    sigma_gate = jax.nn.sigmoid(gate_pre)
    activated = (gate_pre * sigma_gate * up_pre).astype(jnp.bfloat16)
    grad_gate = (back_hidden * up_pre * sigma_gate * (1.0 + gate_pre * (1.0 - sigma_gate))).astype(
        jnp.bfloat16
    )
    grad_up = (back_hidden * gate_pre * sigma_gate).astype(jnp.bfloat16)
    out_part = jnp.einsum(
        "secf,efd->secd", activated, down_mat, preferred_element_type=jnp.float32
    ).astype(jnp.bfloat16)
    grad_part = (
        jnp.einsum("secf,edf->secd", grad_gate, gate_mat, preferred_element_type=jnp.float32)
        + jnp.einsum("secf,edf->secd", grad_up, up_mat, preferred_element_type=jnp.float32)
    ).astype(jnp.bfloat16)
    return (out_part, grad_part)


def body(
    hidden,
    steering,
    norm_gain,
    target,
    routes,
    gate_probs,
    contrast,
    gate_weight,
    up_weight,
    down_weight,
):
    tokens_here, width_here = hidden.shape
    groups = lax.axis_size("dp")
    quarters = lax.axis_size("mp")
    local_experts = gate_weight.shape[0]
    experts_all = local_experts * groups
    top_count = routes.shape[1]
    capacity = min(
        tokens_here, (5 * tokens_here * top_count + 4 * experts_all - 1) // (4 * experts_all)
    )
    pair_count = tokens_here * top_count
    slot_count = experts_all * capacity
    width_full = width_here * quarters
    stream = hidden.astype(jnp.float32) + steering[None, :]
    square_sum = lax.psum(jnp.sum(stream * stream, axis=1), "mp")
    inverse = lax.rsqrt(square_sum / width_full + EPSILON)[:, None]
    gain_row = norm_gain.astype(jnp.float32)[None, :]
    normed = (stream * inverse * gain_row).astype(jnp.bfloat16)
    sign_col = (2 * contrast - 1).astype(jnp.float32)[:, None]
    flat_routes = routes.reshape(-1)
    one_hot = (flat_routes[:, None] == jnp.arange(experts_all, dtype=jnp.int32)[None, :]).astype(
        jnp.int32
    )
    earlier = jnp.cumsum(one_hot, axis=0) - one_hot
    rank_in = jnp.sum(earlier * one_hot, axis=1)
    slot_of = flat_routes * capacity + rank_in
    source = (
        jnp.full((slot_count,), pair_count, jnp.int32)
        .at[slot_of]
        .set(jnp.arange(pair_count, dtype=jnp.int32))
    )
    source_tok = source // top_count
    probs_pad = jnp.concatenate([gate_probs.reshape(-1), jnp.zeros((1,), jnp.float32)])
    slot_probs = probs_pad[source][:, None]
    col_count = normed.shape[1]
    rows_pad = jnp.concatenate([normed, jnp.zeros((1, col_count), jnp.bfloat16)], axis=0)
    cot_pad = jnp.concatenate(
        [target.astype(jnp.float32) * sign_col, jnp.zeros((1, col_count), jnp.float32)], axis=0
    )
    send_rows = rows_pad[source_tok].reshape(groups, local_experts, capacity, col_count)
    send_grad = (
        (cot_pad[source_tok] * slot_probs)
        .astype(jnp.bfloat16)
        .reshape(groups, local_experts, capacity, col_count)
    )
    send_rows, send_grad = (send_rows, send_grad)
    rows_in = lax.all_to_all(send_rows, "dp", split_axis=0, concat_axis=0, tiled=True)
    grad_in = lax.all_to_all(send_grad, "dp", split_axis=0, concat_axis=0, tiled=True)
    zeros_init = jnp.zeros(rows_in.shape[:3] + (gate_weight.shape[2],), jnp.float32)
    rows_piece = lax.all_gather(rows_in, "mp", axis=3, tiled=True)
    grad_piece = lax.all_gather(grad_in, "mp", axis=3, tiled=True)
    partial_terms = expert_inputs(rows_piece, grad_piece, gate_weight, up_weight, down_weight)
    gate_pre, up_pre, back_hidden = jax.tree.map(
        jnp.add, (zeros_init, zeros_init, zeros_init), partial_terms
    )
    out_part, grad_part = expert_outputs(
        gate_pre, up_pre, back_hidden, gate_weight, up_weight, down_weight
    )
    out_share = lax.psum_scatter(
        out_part.astype(jnp.float32).astype(jnp.bfloat16), "mp", scatter_dimension=3, tiled=True
    ).astype(jnp.float32)
    grad_share = lax.psum_scatter(
        grad_part.astype(jnp.float32).astype(jnp.bfloat16), "mp", scatter_dimension=3, tiled=True
    ).astype(jnp.float32)
    back_out = lax.all_to_all(
        out_share.astype(jnp.bfloat16), "dp", split_axis=0, concat_axis=0, tiled=True
    ).astype(out_share.dtype)
    back_grad = lax.all_to_all(
        grad_share.astype(jnp.bfloat16), "dp", split_axis=0, concat_axis=0, tiled=True
    ).astype(grad_share.dtype)
    col_count = back_out.shape[3]
    out_slots = back_out.reshape(slot_count, col_count)[slot_of].reshape(
        tokens_here, top_count, col_count
    )
    grad_slots = back_grad.reshape(slot_count, col_count)[slot_of].reshape(
        tokens_here, top_count, col_count
    )
    out_tok = jnp.sum(out_slots * gate_probs[:, :, None], axis=1)
    grad_tok = jnp.sum(grad_slots, axis=1)
    mixed = (stream + out_tok).astype(jnp.bfloat16)
    project = lax.psum(jnp.sum(stream * gain_row * grad_tok, axis=1), "mp")[:, None]
    cotangent = target.astype(jnp.float32) * sign_col
    grad_stream = (
        cotangent
        + inverse * gain_row * grad_tok
        - stream * inverse * inverse * inverse * project / width_full
    )
    steer_grad = lax.psum(jnp.sum(grad_stream, axis=0), "dp")
    return (mixed, steer_grad)


def solution(mesh):
    placed = (
        P("dp", "mp"),
        P("mp"),
        P("mp"),
        P("dp", "mp"),
        P("dp", None),
        P("dp", None),
        P("dp"),
        P("dp", None, "mp"),
        P("dp", None, "mp"),
        P("dp", "mp", None),
    )
    return jax.shard_map(
        body, mesh=mesh, in_specs=placed, out_specs=(P("dp", "mp"), P("mp")), check_vma=False
    )
```

profile of v0, /device:TPU:0, one launch (start us, length us, event | category | flops | bytes accessed | tf_op | source)
XLA Modules:
  0.0 593.2 jit_solution(3055648589652543636)
XLA Ops:
  13.1 4.1 gather_fusion.2
  17.1 5.2 gather.20
  25.1 4.7 fusion.27
  29.8 7.5 %all-to-all-start.2 = ((bf16[16,1,20,3584]{3,2,1,0:T(8,128)(2,1)}), bf16[16,1,20,3584]{3,2,1,0:T(8,128)(2,1)S(1)}, u32[]{:S(2)}, u32[]{:S(2)}) async-start(bf16[16,1,20,3584]{3,2,1,0:T(8,128)(2,1)} %fusion.27), calls=%async_computation.3 | async-start | bytes 5505024 | tf_op jit(solution)/shard_map/all_to_all | solution.py:93
  37.7 4.9 psum.21
  42.6 47.2 %all-to-all-done.2 = bf16[16,1,20,3584]{3,2,1,0:T(8,128)(2,1)S(1)} async-done(((bf16[16,1,20,3584]{3,2,1,0:T(8,128)(2,1)}), bf16[16,1,20,3584]{3,2,1,0:T(8,128)(2,1)S(1)}, u32[]{:S(2)}, u32[]{:S(2)}) %all-to-all-start.2) | async-done | bytes 2293792 | tf_op jit(solution)/shard_map/all_to_all | solution.py:93
  97.8 77.0 %all_to_all.20 = bf16[16,1,20,3584]{3,2,1,0:T(8,128)(2,1)} all-to-all(bf16[16,1,20,3584]{3,2,1,0:T(8,128)(2,1)S(1)} %bitcast.165), channel_id=1, replica_groups=mesh['dp'=16,'mp'=2] {'dp'}, dimensions={0} | all-to-all | bytes 4587520 | tf_op jit(solution)/shard_map/all_to_all | solution.py:92
  175.1 11.8 %fusion = f32[16,20,1024]{2,1,0:T(8,128)} fusion(bf16[1,1024,7168]{2,1,0:T(8,128)(2,1)} %param.19, bf16[16,1,20,7168]{3,2,0,1:T(8,128)(2,1)} %all-gather.5.cloned.1.call-done), kind=kOutput, calls=%fused_computation.6 | convolution fusion | flops 4697620480 | bytes 20578304 | tf_op jit(solution)/shard_map/secd,efd->secf/dot_general | solution.py:12
  186.9 58.3 %all-gather.3.cloned.1.call-done = bf16[16,1,20,7168]{3,2,0,1:T(8,128)(2,1)} async-done(((bf16[16,1,20,3584]{3,2,0,1:T(8,128)(2,1)}), bf16[16,1,20,7168]{3,2,0,1:T(8,128)(2,1)}) %all-gather.3.cloned.1.call-update) | async-done | bytes 4587536 | tf_op jit(solution)/shard_map/all_gather | solution.py:95
  245.2 10.9 %fusion.10 = f32[16,20,1024]{2,1,0:T(8,128)S(1)} fusion(bf16[1,7168,1024]{2,1,0:T(8,128)(2,1)} %param.17, bf16[16,1,20,7168]{3,2,0,1:T(8,128)(2,1)} %all-gather.3.cloned.1.call-done), kind=kOutput, calls=%fused_computation.16 | convolution fusion | flops 4697620480 | bytes 20578304 | tf_op jit(solution)/shard_map/secd,edf->secf/dot_general | solution.py:10
  256.2 22.0 %fusion.4 = f32[16,20,7168]{2,1,0:T(8,128)} fusion(bf16[1,7168,1024]{2,1,0:T(8,128)(2,1)} %param.18, f32[16,20,1024]{2,1,0:T(8,128)S(1)} %copy-done.7, f32[16,20,1024]{2,1,0:T(8,128)S(1)} %fusion.10), kind=kOutput, calls=%fused_computation.10 | convolution fusion | flops 4699586560 | bytes 26476544 | tf_op jit(solution)/shard_map/secf,edf->secd/dot_general | solution.py:30
  278.2 10.4 %fusion.6 = f32[16,20,1024]{2,1,0:T(8,128)} fusion(bf16[1,7168,1024]{2,1,0:T(8,128)(2,1)} %param.18, bf16[16,1,20,7168]{3,2,0,1:T(8,128)(2,1)S(1)} %copy-done.6), kind=kOutput, calls=%fused_computation.12 | convolution fusion | flops 4697620480 | bytes 20578304 | tf_op jit(solution)/shard_map/secd,edf->secf/dot_general | solution.py:11
  288.6 14.2 %fusion.20 = bf16[16,1,20,7168]{3,2,0,1:T(8,128)(2,1)} fusion(f32[16,20,7168]{2,1,0:T(8,128)} %fusion.4, bf16[1,7168,1024]{2,1,0:T(8,128)(2,1)} %param.17, f32[16,20,1024]{2,1,0:T(8,128)} %fusion, f32[16,20,1024]{2,1,0:T(8,128)} %fusion.6, f32[16,20,1024]{2,1,0:T(8,128)S(1)} %fusion.10), kind=kOutput, calls=%fused_computation.21 | convolution fusion | flops 4705484800 | bytes 32374784 | tf_op jit(solution)/shard_map/secf,edf->secd/dot_general | solution.py:29
  302.8 11.4 %fusion.17 = bf16[16,1,20,7168]{3,2,0,1:T(8,128)(2,1)} fusion(bf16[1,1024,7168]{2,1,0:T(8,128)(2,1)} %param.19, f32[16,20,1024]{2,1,0:T(8,128)} %fusion.6, f32[16,20,1024]{2,1,0:T(8,128)S(1)} %fusion.10), kind=kOutput, calls=%fused_computation.20 | convolution fusion | flops 4701880320 | bytes 21889024 | tf_op jit(solution)/shard_map/secf,efd->secd/dot_general | solution.py:25
  314.3 57.3 %reduce-scatter.5.cloned.1.call-done = bf16[16,1,20,3584]{3,2,0,1:T(8,128)(2,1)} async-done(((bf16[16,1,20,7168]{3,2,0,1:T(8,128)(2,1)}), bf16[16,1,20,3584]{3,2,0,1:T(8,128)(2,1)}) %reduce-scatter.5.cloned.1.call-update) | async-done | bytes 2293776 | tf_op jit(solution)/shard_map/reduce_scatter | solution.py:107
  371.6 5.6 all-to-all-start.3
  377.2 65.2 %reduce-scatter.3.cloned.1.call-done = bf16[16,1,20,3584]{3,2,0,1:T(8,128)(2,1)} async-done(((bf16[16,1,20,7168]{3,2,0,1:T(8,128)(2,1)}), bf16[16,1,20,3584]{3,2,0,1:T(8,128)(2,1)}) %reduce-scatter.3.cloned.1.call-update) | async-done | bytes 2293776 | tf_op jit(solution)/shard_map/reduce_scatter | solution.py:104
  442.3 5.7 all-to-all-start.1
  450.7 7.5 %gather_fusion.4 = f32[256,3584]{1,0:T(8,128)} fusion(f32[320,3584]{1,0:T(8,128)} %reshape.159, s32[1024]{0:T(1024)S(1)} %pad_clamp_fusion.1), kind=kCustom, calls=%fused_computation.4 | custom fusion | bytes 7341056 | tf_op jit(solution)/shard_map/gather | solution.py:120
  461.3 4.9 psum.22
  466.3 34.2 %all-to-all-done.1 = bf16[16,1,20,3584]{3,2,1,0:T(8,128)(2,1)} async-done(((bf16[16,1,20,3584]{3,2,1,0:T(8,128)(2,1)}), bf16[16,1,20,3584]{3,2,1,0:T(8,128)(2,1)}, u32[]{:S(2)}, u32[]{:S(2)}) %all-to-all-start.1) | async-done | bytes 2293792 | tf_op jit(solution)/shard_map/all_to_all | solution.py:110
  500.5 4.5 reshape.157
  505.0 7.5 %gather_fusion.1 = f32[256,3584]{1,0:T(8,128)} fusion(f32[320,3584]{1,0:T(8,128)} %reshape.157, s32[1024]{0:T(1024)S(1)} %pad_clamp_fusion.1), kind=kCustom, calls=%fused_computation.1 | custom fusion | bytes 7341056 | tf_op jit(solution)/shard_map/gather | solution.py:117
  516.7 70.0 %psum.23 = f32[3584]{0:T(1024)} all-reduce(f32[3584]{0:T(1024)S(1)} %get-tuple-element.2), channel_id=1, replica_groups=mesh['dp'=16,'mp'=2] {'dp'}, use_global_device_ids=true, to_apply=%region_13.14 | all-reduce | flops 3584 | bytes 28672 | tf_op jit(solution)/shard_map/psum | solution.py:133
  (64 shorter events, 27.2 us)
Async XLA Ops:
  17.1 5.2 copy-start.5
  29.8 7.6 %copy-start.4 = (bf16[3584]{0:T(1024)(128)(2,1)S(1)}, bf16[3584]{0:T(1024)(128)(2,1)}, u32[]{:S(2)}) copy-start(bf16[3584]{0:T(1024)(128)(2,1)} %param.12) | copy-start | bytes 21508
  29.8 7.6 %copy-start.1 = (bf16[32,3584]{1,0:T(8,128)(2,1)S(1)}, bf16[32,3584]{1,0:T(8,128)(2,1)}, u32[]{:S(2)}) copy-start(bf16[32,3584]{1,0:T(8,128)(2,1)} %param.10) | copy-start | bytes 688132
  29.8 7.6 %copy-start.3 = (f32[3584]{0:T(1024)S(1)}, f32[3584]{0:T(1024)}, u32[]{:S(2)}) copy-start(f32[3584]{0:T(1024)} %param.11) | copy-start | bytes 43012
  29.8 59.9 %all-to-all-start.2 = ((bf16[16,1,20,3584]{3,2,1,0:T(8,128)(2,1)}), bf16[16,1,20,3584]{3,2,1,0:T(8,128)(2,1)S(1)}, u32[]{:S(2)}, u32[]{:S(2)}) async-start(bf16[16,1,20,3584]{3,2,1,0:T(8,128)(2,1)} %fusion.27), calls=%async_computation.3 | async-start | bytes 5505024 | tf_op jit(solution)/shard_map/all_to_all | solution.py:93
  37.4 137.7 %all-gather.5.cloned.1.call-start = ((), (), s32[]{:S(2)}) async-start(), calls=%async_computation.8 | async-start | bytes 8257536 | tf_op jit(solution)/shard_map/all_gather | solution.py:96
  89.8 1.5 copy-start
  91.3 153.9 %all-gather.3.cloned.1.call-start = ((), (), s32[]{:S(2)}) async-start(), calls=%async_computation.6 | async-start | bytes 8257536 | tf_op jit(solution)/shard_map/all_gather | solution.py:95
  174.8 196.8 %reduce-scatter.5.cloned.1.call-start = ((), (), s32[]{:S(2)}) async-start(), calls=%async_computation.9 | async-start | bytes 8257536 | tf_op jit(solution)/shard_map/reduce_scatter | solution.py:107
  245.2 10.9 %copy-start.7 = (f32[16,20,1024]{2,1,0:T(8,128)S(1)}, f32[16,20,1024]{2,1,0:T(8,128)}, u32[]{:S(2)}) copy-start(f32[16,20,1024]{2,1,0:T(8,128)} %fusion) | copy-start | bytes 3932164
  256.2 22.0 %copy-start.6 = (bf16[16,1,20,7168]{3,2,0,1:T(8,128)(2,1)S(1)}, bf16[16,1,20,7168]{3,2,0,1:T(8,128)(2,1)}, u32[]{:S(2)}) copy-start(bf16[16,1,20,7168]{3,2,0,1:T(8,128)(2,1)} %all-gather.3.cloned.1.call-done) | copy-start | bytes 13762564
  302.8 139.6 %reduce-scatter.3.cloned.1.call-start = ((), (), s32[]{:S(2)}) async-start(), calls=%async_computation.7 | async-start | bytes 8257536 | tf_op jit(solution)/shard_map/reduce_scatter | solution.py:104
  371.6 70.8 %all-to-all-start.3 = ((bf16[16,1,20,3584]{3,2,1,0:T(8,128)(2,1)}), bf16[16,1,20,3584]{3,2,1,0:T(8,128)(2,1)S(1)}, u32[]{:S(2)}, u32[]{:S(2)}) async-start(bf16[16,1,20,3584]{3,2,1,0:T(8,128)(2,1)} %bitcast.167), calls=%async_computation.5 | async-start | bytes 5505024 | tf_op jit(solution)/shard_map/all_to_all | solution.py:113
  442.3 58.1 %all-to-all-start.1 = ((bf16[16,1,20,3584]{3,2,1,0:T(8,128)(2,1)}), bf16[16,1,20,3584]{3,2,1,0:T(8,128)(2,1)}, u32[]{:S(2)}, u32[]{:S(2)}) async-start(bf16[16,1,20,3584]{3,2,1,0:T(8,128)(2,1)} %bitcast.166), calls=%async_computation.2 | async-start | bytes 5505024 | tf_op jit(solution)/shard_map/all_to_all | solution.py:110
  512.4 3.3 copy-start.2
Sparse Core Ops, SparseCore 0:
  91.4 80.6 all-gather.4
  174.9 70.2 all-gather.2
  302.9 68.6 reduce-scatter.4
  373.7 68.5 reduce-scatter.2
where the time goes:
time: 594 us; the launch traced here: 593 us
  waiting for transfers between devices  262 us (44%)
  blocking collectives  157 us (26%)
  matrix products  80.7 us (14%)
  local copies, waits for them, and re-layouts  44.6 us (8%)
  starting transfers between devices  19.2 us (3%)
  other arithmetic  15.6 us (3%)
  between operations  14 us (2%)
    all_to_all x1, blocking collectives, body(): lax.all_to_all(send_rows, 'dp', split_axis=0, concat_axis=0, tiled=True)  77 us
    psum x1, blocking collectives, body(): steer_grad = lax.psum(jnp.sum(grad_stream, axis=0), 'dp')  70 us
    reduce_scatter x1, waiting for transfers between devices, body(): lax.psum_scatter(out_part.astype(jnp.float32).astype(jnp.bfloat16), 'mp',...  65.2 us
    all_gather x1, waiting for transfers between devices, body(): rows_piece = lax.all_gather(rows_in, 'mp', axis=3, tiled=True)  58.3 us
    reduce_scatter x1, waiting for transfers between devices, body(): lax.psum_scatter(grad_part.astype(jnp.float32).astype(jnp.bfloat16), 'mp'...  57.3 us
    all_to_all x1, waiting for transfers between devices, body(): lax.all_to_all(send_grad, 'dp', split_axis=0, concat_axis=0, tiled=True)  47.2 us
    all_to_all x1, waiting for transfers between devices, body(): lax.all_to_all(out_share.astype(jnp.bfloat16), 'dp', split_axis=0, concat...  34.2 us
    dot_general x1, matrix products, expert_outputs(): jnp.einsum('secf,edf->secd', grad_up, up_mat, preferred_element_type=jnp....  22 us
  transfers between devices with their start and end apart: 7, of which 5 were waited for; matrix products, arithmetic and copies ran while one was open for 7% of the time, Pallas kernels for 0%

commit v1 on v0

--- a/solution.py
+++ b/solution.py
@@ -92,7 +92,7 @@
     rows_in = lax.all_to_all(send_rows, "dp", split_axis=0, concat_axis=0, tiled=True)
     grad_in = lax.all_to_all(send_grad, "dp", split_axis=0, concat_axis=0, tiled=True)
     zeros_init = jnp.zeros(rows_in.shape[:3] + (gate_weight.shape[2],), jnp.float32)
-    rows_piece = lax.all_gather(rows_in, "mp", axis=3, tiled=True)
+    rows_piece = jnp.concatenate(lax.all_gather(rows_in, "mp"), axis=3)
     grad_piece = lax.all_gather(grad_in, "mp", axis=3, tiled=True)
     partial_terms = expert_inputs(rows_piece, grad_piece, gate_weight, up_weight, down_weight)
     gate_pre, up_pre, back_hidden = jax.tree.map(

time: 594 us -> 575 us (0.968)
  waiting for transfers between devices: 262 us -> 219 us
  local copies, waits for them, and re-layouts: 44.6 us -> 64.8 us
    all_gather x1, waiting for transfers between devices: 58.3 us -> 0.02 us  [body(): rows_piece = jnp.concatenate(lax.all_gather(rows_in, 'mp'), axis=3)]
    all_gather x1, waiting for transfers between devices: 0.02 us -> 42.4 us  [body(): grad_piece = lax.all_gather(grad_in, 'mp', axis=3, tiled=True)]
    all_to_all x1, waiting for transfers between devices: 0.01 us -> 39.1 us  [body(): lax.all_to_all(grad_share.astype(jnp.bfloat16), 'dp', split_axis=0, conca...]
    all_to_all x1, waiting for transfers between devices: 34.2 us -> 0.01 us  [body(): lax.all_to_all(out_share.astype(jnp.bfloat16), 'dp', split_axis=0, concat...]
    reduce_scatter x1, waiting for transfers between devices: 65.2 us -> 34 us  [body(): lax.psum_scatter(out_part.astype(jnp.float32).astype(jnp.bfloat16), 'mp',...]
    dot_general x1, matrix products: 22 us -> 11.9 us  [expert_outputs(): jnp.einsum('secf,edf->secd', grad_up, up_mat, preferred_element_type=jnp....]
    reshape x0 -> x1, local copies, waits for them, and re-layouts: none -> 9.22 us  [body(): rows_piece = jnp.concatenate(lax.all_gather(rows_in, 'mp'), axis=3)]
    all_to_all x1, waiting for transfers between devices: 47.2 us -> 38.2 us  [body(): lax.all_to_all(send_rows, 'dp', split_axis=0, concat_axis=0, tiled=True)]
  transfers between devices with their start and end apart: 7 -> 7, of which waited for: 5 -> 5; matrix products, arithmetic and copies ran while one was open for 7% -> 16% of each run, Pallas kernels for 0% -> 0%
where the time goes in v1:
time: 575 us; the launch traced here: 568 us
  waiting for transfers between devices  219 us (38%)
  blocking collectives  157 us (27%)
  matrix products  79.8 us (14%)
  local copies, waits for them, and re-layouts  64.8 us (11%)
  starting transfers between devices  18.7 us (3%)
  other arithmetic  15.6 us (3%)
  between operations  14.3 us (2%)
    all_to_all x1, blocking collectives, body(): lax.all_to_all(send_grad, 'dp', split_axis=0, concat_axis=0, tiled=True)  77 us
    psum x1, blocking collectives, body(): steer_grad = lax.psum(jnp.sum(grad_stream, axis=0), 'dp')  68.8 us
    reduce_scatter x1, waiting for transfers between devices, body(): lax.psum_scatter(grad_part.astype(jnp.float32).astype(jnp.bfloat16), 'mp'...  65 us
    all_gather x1, waiting for transfers between devices, body(): grad_piece = lax.all_gather(grad_in, 'mp', axis=3, tiled=True)  42.4 us
    all_to_all x1, waiting for transfers between devices, body(): lax.all_to_all(grad_share.astype(jnp.bfloat16), 'dp', split_axis=0, conca...  39.1 us
    all_to_all x1, waiting for transfers between devices, body(): lax.all_to_all(send_rows, 'dp', split_axis=0, concat_axis=0, tiled=True)  38.2 us
    reduce_scatter x1, waiting for transfers between devices, body(): lax.psum_scatter(out_part.astype(jnp.float32).astype(jnp.bfloat16), 'mp',...  34 us
    dot_general x1, matrix products, expert_outputs(): jnp.einsum('secf,edf->secd', grad_gate, gate_mat, preferred_element_type=...  22.7 us
  transfers between devices with their start and end apart: 7, of which 5 were waited for; matrix products, arithmetic and copies ran while one was open for 16% of the time, Pallas kernels for 0%

profile of v1, /device:TPU:0, one launch (start us, length us, event | category | flops | bytes accessed | tf_op | source)
XLA Modules:
  0.0 568.5 jit_solution(4698016876754996257)
XLA Ops:
  9.9 5.9 %psum.21 = f32[32]{0:T(128)S(1)} all-reduce(f32[32]{0:T(128)S(1)} %multiply_reduce_fusion.1), channel_id=1, replica_groups=mesh['dp'=16,'mp'=2] {'mp'}, use_global_device_ids=true, to_apply=%region_1.0 | all-reduce | flops 32 | bytes 256 | tf_op jit(solution)/shard_map/psum | solution.py:60
  26.7 6.6 %all-to-all-start = ((bf16[16,1,20,3584]{3,2,1,0:T(8,128)(2,1)}), bf16[16,1,20,3584]{3,2,1,0:T(8,128)(2,1)S(1)}, u32[]{:S(2)}, u32[]{:S(2)}) async-start(bf16[16,1,20,3584]{3,2,1,0:T(8,128)(2,1)} %bitcast.129), calls=%async_computation | async-start | bytes 5505024 | tf_op jit(solution)/shard_map/all_to_all | solution.py:92
  42.2 5.2 gather.20
  47.4 38.2 %all-to-all-done = bf16[16,1,20,3584]{3,2,1,0:T(8,128)(2,1)S(1)} async-done(((bf16[16,1,20,3584]{3,2,1,0:T(8,128)(2,1)}), bf16[16,1,20,3584]{3,2,1,0:T(8,128)(2,1)S(1)}, u32[]{:S(2)}, u32[]{:S(2)}) %all-to-all-start) | async-done | bytes 2293792 | tf_op jit(solution)/shard_map/all_to_all | solution.py:92
  91.0 77.0 %all_to_all.20 = bf16[16,1,20,3584]{3,2,1,0:T(8,128)(2,1)} all-to-all(bf16[16,1,20,3584]{3,2,1,0:T(8,128)(2,1)S(1)} %fusion.25), channel_id=1, replica_groups=mesh['dp'=16,'mp'=2] {'dp'}, dimensions={0} | all-to-all | bytes 4587520 | tf_op jit(solution)/shard_map/all_to_all | solution.py:93
  168.4 9.2 %copy.29 = bf16[16,1,20,2,3584]{4,3,0,2,1:T(2,128)(2,1)} copy(bf16[16,1,20,2,3584]{4,0,3,2,1:T(8,128)(2,1)} %bitcast.131) | data formatting | bytes 9175040 | tf_op jit(solution)/shard_map/reshape | solution.py:95
  177.6 8.8 %reshape.148 = bf16[16,20,7168]{2,0,1:T(8,128)(2,1)} reshape(bf16[16,1,20,2,3584]{4,3,0,2,1:T(2,128)(2,1)} %copy.29) | data formatting | bytes 9175040 | tf_op jit(solution)/shard_map/reshape.4
  186.4 9.6 %fusion.26 = f32[16,1,20,1024]{3,0,2,1:T(8,128)S(1)} fusion(bf16[16,20,7168]{2,0,1:T(8,128)(2,1)} %reshape.148, bf16[1,7168,1024]{2,1,0:T(8,128)(2,1)} %param.17), kind=kOutput, calls=%fused_computation.28 | convolution fusion | flops 4697620480 | bytes 20578304 | tf_op jit(solution)/shard_map/secd,edf->secf/dot_general | solution.py:10
  196.0 42.4 %all-gather.4.cloned.1.call-done = bf16[16,1,20,7168]{3,2,0,1:T(8,128)(2,1)} async-done(((bf16[16,1,20,3584]{3,2,0,1:T(8,128)(2,1)}), bf16[16,1,20,7168]{3,2,0,1:T(8,128)(2,1)}) %all-gather.4.cloned.1.call-update) | async-done | bytes 4587536 | tf_op jit(solution)/shard_map/all_gather | solution.py:96
  238.4 10.9 %fusion = f32[16,20,1024]{2,1,0:T(8,128)S(1)} fusion(bf16[1,1024,7168]{2,1,0:T(8,128)(2,1)} %param.19, bf16[16,1,20,7168]{3,2,0,1:T(8,128)(2,1)} %all-gather.4.cloned.1.call-done), kind=kOutput, calls=%fused_computation.6 | convolution fusion | flops 4697620480 | bytes 20578304 | tf_op jit(solution)/shard_map/secd,efd->secf/dot_general | solution.py:12
  249.3 11.1 %fusion.42 = (bf16[16,20,1024]{2,0,1:T(8,128)(2,1)S(1)}, bf16[16,20,1024]{2,0,1:T(8,128)(2,1)S(1)}, bf16[16,20,1024]{2,0,1:T(8,128)(2,1)S(1)}) fusion(f32[16,1,20,1024]{3,0,2,1:T(8,128)S(1)} %fusion.26, f32[16,20,1024]{2,1,0:T(8,128)S(1)} %fusion, bf16[16,20,7168]{2,0,1:T(8,128)(2,1)S(1)} %copy-done, bf16[1,7168,1024]{2,1,0:T(8,128)(2,1)} %param.18), kind=kOutput, calls=%fused_computation.44 | convolution fusion | flops 4702863360 | bytes 23855104 | tf_op jit(solution)/shard_map/secd,edf->secf/dot_general | solution.py:11
  260.4 13.5 %fusion.17 = bf16[16,1,20,7168]{3,2,0,1:T(8,128)(2,1)} fusion(bf16[1,1024,7168]{2,1,0:T(8,128)(2,1)} %param.19, bf16[16,20,1024]{2,0,1:T(8,128)(2,1)S(1)} %get-tuple-element.4), kind=kOutput, calls=%fused_computation.20 | convolution fusion | flops 4699914240 | bytes 19922944 | tf_op jit(solution)/shard_map/secf,efd->secd/dot_general | solution.py:25
  274.0 11.9 %fusion.4 = f32[16,20,7168]{2,1,0:T(8,128)} fusion(bf16[1,7168,1024]{2,1,0:T(8,128)(2,1)} %param.18, bf16[16,20,1024]{2,0,1:T(8,128)(2,1)S(1)} %get-tuple-element.3), kind=kOutput, calls=%fused_computation.10 | convolution fusion | flops 4697620480 | bytes 24510464 | tf_op jit(solution)/shard_map/secf,edf->secd/dot_general | solution.py:30
  285.9 22.7 %fusion.20 = bf16[16,1,20,7168]{3,2,0,1:T(8,128)(2,1)} fusion(f32[16,20,7168]{2,1,0:T(8,128)} %fusion.4, bf16[1,7168,1024]{2,1,0:T(8,128)(2,1)} %param.17, bf16[16,20,1024]{2,0,1:T(8,128)(2,1)S(1)} %get-tuple-element.2), kind=kOutput, calls=%fused_computation.21 | convolution fusion | flops 4702208000 | bytes 29097984 | tf_op jit(solution)/shard_map/secf,edf->secd/dot_general | solution.py:29
  308.7 34.0 %reduce-scatter.3.cloned.1.call-done = bf16[16,1,20,3584]{3,2,0,1:T(8,128)(2,1)} async-done(((bf16[16,1,20,7168]{3,2,0,1:T(8,128)(2,1)}), bf16[16,1,20,3584]{3,2,0,1:T(8,128)(2,1)}) %reduce-scatter.3.cloned.1.call-update) | async-done | bytes 2293776 | tf_op jit(solution)/shard_map/reduce_scatter | solution.py:104
  342.7 5.8 %all-to-all-start.1 = ((bf16[16,1,20,3584]{3,2,1,0:T(8,128)(2,1)}), bf16[16,1,20,3584]{3,2,1,0:T(8,128)(2,1)S(1)}, u32[]{:S(2)}, u32[]{:S(2)}) async-start(bf16[16,1,20,3584]{3,2,1,0:T(8,128)(2,1)} %bitcast.133), calls=%async_computation.2 | async-start | bytes 5505024 | tf_op jit(solution)/shard_map/all_to_all | solution.py:110
  348.4 65.0 %reduce-scatter.5.cloned.1.call-done = bf16[16,1,20,3584]{3,2,0,1:T(8,128)(2,1)} async-done(((bf16[16,1,20,7168]{3,2,0,1:T(8,128)(2,1)}), bf16[16,1,20,3584]{3,2,0,1:T(8,128)(2,1)}) %reduce-scatter.5.cloned.1.call-update) | async-done | bytes 2293776 | tf_op jit(solution)/shard_map/reduce_scatter | solution.py:107
  413.5 5.9 %all-to-all-start.3 = ((bf16[16,1,20,3584]{3,2,1,0:T(8,128)(2,1)}), bf16[16,1,20,3584]{3,2,1,0:T(8,128)(2,1)}, u32[]{:S(2)}, u32[]{:S(2)}) async-start(bf16[16,1,20,3584]{3,2,1,0:T(8,128)(2,1)} %bitcast.132), calls=%async_computation.5 | async-start | bytes 5505024 | tf_op jit(solution)/shard_map/all_to_all | solution.py:113
  422.0 7.5 %gather_fusion.1 = f32[256,3584]{1,0:T(8,128)} fusion(f32[320,3584]{1,0:T(8,128)} %reshape.164, s32[1024]{0:T(1024)S(1)} %pad_clamp_fusion.1), kind=kCustom, calls=%fused_computation.1 | custom fusion | bytes 7341056 | tf_op jit(solution)/shard_map/gather | solution.py:117
  432.7 39.1 %all-to-all-done.3 = bf16[16,1,20,3584]{3,2,1,0:T(8,128)(2,1)} async-done(((bf16[16,1,20,3584]{3,2,1,0:T(8,128)(2,1)}), bf16[16,1,20,3584]{3,2,1,0:T(8,128)(2,1)}, u32[]{:S(2)}, u32[]{:S(2)}) %all-to-all-start.3) | async-done | bytes 2293792 | tf_op jit(solution)/shard_map/all_to_all | solution.py:113
  471.8 4.5 reshape.166
  476.3 7.5 %gather_fusion.4 = f32[256,3584]{1,0:T(8,128)} fusion(f32[320,3584]{1,0:T(8,128)} %reshape.166, s32[1024]{0:T(1024)S(1)} %pad_clamp_fusion.1), kind=kCustom, calls=%fused_computation.4 | custom fusion | bytes 7341056 | tf_op jit(solution)/shard_map/gather | solution.py:120
  487.0 5.0 psum.22
  492.9 68.8 %psum.23 = f32[3584]{0:T(1024)} all-reduce(f32[3584]{0:T(1024)S(1)} %get-tuple-element.5), channel_id=1, replica_groups=mesh['dp'=16,'mp'=2] {'dp'}, use_global_device_ids=true, to_apply=%region_13.14 | all-reduce | flops 3584 | bytes 28672 | tf_op jit(solution)/shard_map/psum | solution.py:133
  (89 shorter events, 38.2 us)
Async XLA Ops:
  15.8 4.4 copy-start.14
  16.7 3.5 copy-start.3
  20.2 4.2 copy-start.9
  24.4 8.9 %copy-start.11 = (f32[32,8]{0,1:T(8,128)S(1)}, f32[32,8]{0,1:T(8,128)}, u32[]{:S(2)}) copy-start(f32[32,8]{0,1:T(8,128)} %param.15) | copy-start | bytes 3076
  24.4 9.7 %copy-start.10 = (s32[1024]{0:T(1024)S(1)}, s32[1024]{0:T(1024)}, u32[]{:S(2)}) copy-start(s32[1024]{0:T(1024)} %get-tuple-element.9) | copy-start | bytes 12292
  26.7 10.6 %copy-start.18 = (s32[32]{0:T(128)S(1)}, s32[32]{0:T(128)}, u32[]{:S(2)}) copy-start(s32[32]{0:T(128)} %param.16) | copy-start | bytes 388
  26.7 11.2 %copy-start.2 = (bf16[32,3584]{1,0:T(8,128)(2,1)S(1)}, bf16[32,3584]{1,0:T(8,128)(2,1)}, u32[]{:S(2)}) copy-start(bf16[32,3584]{1,0:T(8,128)(2,1)} %param.13) | copy-start | bytes 688132
  26.7 59.0 %all-to-all-start = ((bf16[16,1,20,3584]{3,2,1,0:T(8,128)(2,1)}), bf16[16,1,20,3584]{3,2,1,0:T(8,128)(2,1)S(1)}, u32[]{:S(2)}, u32[]{:S(2)}) async-start(bf16[16,1,20,3584]{3,2,1,0:T(8,128)(2,1)} %bitcast.129), calls=%async_computation | async-start | bytes 5505024 | tf_op jit(solution)/shard_map/all_to_all | solution.py:92
  33.3 135.1 %all-gather.6.cloned.1.call-start = ((), (), s32[]{:S(2)}) async-start(), calls=%async_computation.9 | async-start | bytes 6881280 | tf_op jit(solution)/shard_map/all_gather | solution.py:95
  33.4 0.6 copy-start.6
  47.4 40.4 %copy-start.8 = (f32[16,20]{1,0:T(8,128)S(1)}, f32[16,20]{1,0:T(8,128)}, u32[]{:S(2)}) copy-start(f32[16,20]{1,0:T(8,128)} %mul.168) | copy-start | bytes 3844
  87.7 150.6 %all-gather.4.cloned.1.call-start = ((), (), s32[]{:S(2)}) async-start(), calls=%async_computation.7 | async-start | bytes 8257536 | tf_op jit(solution)/shard_map/all_gather | solution.py:96
  168.0 174.7 %reduce-scatter.3.cloned.1.call-start = ((), (), s32[]{:S(2)}) async-start(), calls=%async_computation.6 | async-start | bytes 8257536 | tf_op jit(solution)/shard_map/reduce_scatter | solution.py:104
  238.4 10.9 %copy-start = (bf16[16,20,7168]{2,0,1:T(8,128)(2,1)S(1)}, bf16[16,20,7168]{2,0,1:T(8,128)(2,1)}, u32[]{:S(2)}) copy-start(bf16[16,20,7168]{2,0,1:T(8,128)(2,1)} %reshape.148) | copy-start | bytes 13762564
  273.9 139.6 %reduce-scatter.5.cloned.1.call-start = ((), (), s32[]{:S(2)}) async-start(), calls=%async_computation.8 | async-start | bytes 8257536 | tf_op jit(solution)/shard_map/reduce_scatter | solution.py:107
  342.7 76.7 %copy-start.13 = (s32[256,1]{0,1:T(1,128)S(1)}, s32[256,1]{0,1:T(1,128)}, u32[]{:S(2)}) copy-start(s32[256,1]{0,1:T(1,128)} %copy-done.12) | copy-start | bytes 3076
  342.7 70.8 %all-to-all-start.1 = ((bf16[16,1,20,3584]{3,2,1,0:T(8,128)(2,1)}), bf16[16,1,20,3584]{3,2,1,0:T(8,128)(2,1)S(1)}, u32[]{:S(2)}, u32[]{:S(2)}) async-start(bf16[16,1,20,3584]{3,2,1,0:T(8,128)(2,1)} %bitcast.133), calls=%async_computation.2 | async-start | bytes 5505024 | tf_op jit(solution)/shard_map/all_to_all | solution.py:110
  413.5 58.4 %all-to-all-start.3 = ((bf16[16,1,20,3584]{3,2,1,0:T(8,128)(2,1)}), bf16[16,1,20,3584]{3,2,1,0:T(8,128)(2,1)}, u32[]{:S(2)}, u32[]{:S(2)}) async-start(bf16[16,1,20,3584]{3,2,1,0:T(8,128)(2,1)} %bitcast.132), calls=%async_computation.5 | async-start | bytes 5505024 | tf_op jit(solution)/shard_map/all_to_all | solution.py:113
  422.0 7.5 %copy-start.7 = (f32[32,8]{1,0:T(8,128)S(1)}, f32[32,8]{1,0:T(8,128)}, u32[]{:S(2)}) copy-start(f32[32,8]{1,0:T(8,128)} %copy-done.6) | copy-start | bytes 3076
  476.3 10.5 %copy-start.1 = (bf16[32,3584]{1,0:T(8,128)(2,1)S(1)}, bf16[32,3584]{1,0:T(8,128)(2,1)}, u32[]{:S(2)}) copy-start(bf16[32,3584]{1,0:T(8,128)(2,1)} %param.10) | copy-start | bytes 688132
  476.3 10.5 %copy-start.4 = (f32[3584]{0:T(1024)S(1)}, f32[3584]{0:T(1024)}, u32[]{:S(2)}) copy-start(f32[3584]{0:T(1024)} %copy-done.3) | copy-start | bytes 43012
  476.3 10.5 %copy-start.5 = (f32[3584]{0:T(1024)S(1)}, f32[3584]{0:T(1024)}, u32[]{:S(2)}) copy-start(f32[3584]{0:T(1024)} %param.11) | copy-start | bytes 43012
  483.8 8.2 %copy-start.15 = (f32[32]{0:T(128)S(1)}, f32[32]{0:T(128)}, u32[]{:S(2)}) copy-start(f32[32]{0:T(128)} %copy-done.14) | copy-start | bytes 388
  483.8 8.2 %copy-start.17 = (f32[32]{0:T(128)S(1)}, f32[32]{0:T(128)}, u32[]{:S(2)}) copy-start(f32[32]{0:T(128)} %copy-done.16) | copy-start | bytes 388
  (2 other events, 1.2 us)
Sparse Core Ops, SparseCore 0:
  87.9 70.3 all-gather.5
  168.1 70.1 all-gather.3
  274.0 68.6 reduce-scatter.2
  344.8 68.5 reduce-scatter.4
